TPU v7x, 32 devices: a whole 2x2x4 slice. The times are simulated.
32 devices in a mesh: dp: 32 (over z, y, x, core), tensor: 1.
Axes of the slice: x: 2, y: 2, z: 4, core: 2. Of those that a mesh axis runs over, the one named last changes fastest.
Arguments:
- latent_raw: bfloat16 [6144, 512], P('dp'), may hold values from -6 to 6
- norm_gain: float32 [512], replicated, may hold values from 0.5 to 1.5
- up_weight: bfloat16 [512, 4096], P(None, 'tensor'), may hold values from -0.25 to 0.25
- grad_kv: bfloat16 [6144, 4096], P('dp', 'tensor'), may hold values from -3 to 3
Outputs:
- latent_grad: bfloat16 [6144, 512], P('dp')
- gain_grad: float32 [512], replicated
- weight_grad: float32 [512, 4096], P('dp', 'tensor')
All inputs are finite; a program needn't handle non-finite values.
Results may differ from a plain program's by a relative error of at most 0.0029.
Values may be sent and summed in bfloat16 or wider, within the bound.
A program may use at most 64 MiB of HBM per device.

v0:
```python
import jax
import jax.numpy as jnp
from jax import lax
from jax.sharding import PartitionSpec as P

epsilon = 1e-06


def normalize(latent_raw):
    latent_full = latent_raw.astype(jnp.float32)
    inverse = lax.rsqrt(jnp.mean(latent_full * latent_full, axis=-1, keepdims=True) + epsilon)
    return (latent_full * inverse, inverse)


def norm_backward(grad_norm, scaled_rows, inverse, norm_gain):
    upstream = grad_norm * norm_gain
    centred = upstream - scaled_rows * jnp.mean(upstream * scaled_rows, axis=-1, keepdims=True)
    return (inverse * centred).astype(jnp.bfloat16)


def per_device(latent_raw, norm_gain, up_weight, grad_kv):
    scaled_rows, inverse = normalize(latent_raw)
    normed = (scaled_rows * norm_gain).astype(jnp.bfloat16)
    factor = float(latent_raw.shape[0] * lax.axis_size("dp")) ** (-0.5)
    partial_norm = lax.dot_general(
        grad_kv, up_weight, (((1,), (1,)), ((), ())), preferred_element_type=jnp.float32
    )
    grad_norm = lax.psum_scatter(partial_norm, "tensor", scatter_dimension=0, tiled=True)
    row_count = grad_norm.shape[0]
    offset = lax.axis_index("tensor") * row_count
    scaled_part = lax.dynamic_slice_in_dim(scaled_rows, offset, row_count, 0)
    inverse_part = lax.dynamic_slice_in_dim(inverse, offset, row_count, 0)
    gain_local = jnp.sum(grad_norm * scaled_part, axis=0)
    latent_part = norm_backward(grad_norm, scaled_part, inverse_part, norm_gain)
    latent_grad = lax.all_gather(latent_part, "tensor", axis=0, tiled=True)
    gain_grad = lax.psum(gain_local, ("dp", "tensor")) * factor
    weight_partial = lax.dot_general(
        normed, grad_kv, (((0,), (0,)), ((), ())), preferred_element_type=jnp.float32
    )
    weight_grad = lax.psum_scatter(weight_partial, "dp", scatter_dimension=0, tiled=True) * factor
    return (latent_grad, gain_grad, weight_grad)


def solution(mesh):
    in_specs = (P("dp", None), P(), P(None, "tensor"), P("dp", "tensor"))
    out_specs = (P("dp", None), P(), P("dp", "tensor"))
    return jax.shard_map(
        per_device, mesh=mesh, in_specs=in_specs, out_specs=out_specs, check_vma=False
    )
```

profile of v0, /device:TPU:0, one launch (start us, length us, event | category | flops | bytes accessed | tf_op | source)
XLA Modules:
  0.0 175.9 jit_solution(13392894614203619147)
XLA Ops:
  7.2 0.0 copy-start
  7.2 0.0 reduce-scatter.2.cloned.1.call-start
  7.2 1.2 fusion.10
  8.4 0.3 copy-done
  8.7 5.5 %fusion.11 = f32[512,4096]{1,0:T(8,128)} fusion(bf16[192,4096]{1,0:T(8,128)(2,1)S(1)} %copy-done, bf16[192,512]{1,0:T(8,128)(2,1)} %param.4, f32[512]{0:T(512)} %param.5, f32[192]{0:T(256)S(1)} %add_rsqrt_fusion), kind=kOutput, calls=%fused_computation.13 | convolution fusion | flops 805699584 | bytes 10160896 | tf_op jit(solution)/shard_map/dot_general | solution.py:37
  14.2 0.0 copy-start.1
  14.2 0.0 copy-start.2
  14.2 0.0 reduce-scatter.2.cloned.1.call-update
  14.2 0.9 copy-done.1
  15.1 0.0 copy-done.2
  15.1 3.8 %fusion.8 = (f32[512]{0:T(512)S(1)}, f32[192]{0:T(256)S(1)}, f32[192,512]{1,0:T(8,128)S(1)}) fusion(bf16[192,512]{1,0:T(8,128)(2,1)S(1)} %copy-done.1, f32[192]{0:T(256)S(1)} %add_rsqrt_fusion, f32[512]{0:T(512)S(1)} %copy-done.2, bf16[192,4096]{1,0:T(8,128)(2,1)S(1)} %copy-done, bf16[512,4096]{1,0:T(8,128)(2,1)} %param.6), kind=kOutput, calls=%fused_computation.10 | convolution fusion | flops 805993792 | bytes 6362624 | tf_op jit(solution)/shard_map/dot_general | solution.py:25
  19.0 44.0 %psum.7 = f32[512]{0:T(512)S(1)} all-reduce(f32[512]{0:T(512)S(1)} %get-tuple-element.3), channel_id=1, replica_groups=mesh['dp'=32,'tensor'=1] {'dp','tensor'}, use_global_device_ids=true, to_apply=%region_3.0 | all-reduce | flops 512 | bytes 4096 | tf_op jit(solution)/shard_map/psum | solution.py:36
  63.0 0.6 broadcast_multiply_fusion.1
  63.6 0.9 fusion.7
  64.4 103.0 %reduce-scatter.2.cloned.1.call-done = f32[16,4096]{1,0:T(8,128)} async-done(((f32[512,4096]{1,0:T(8,128)}), f32[16,4096]{1,0:T(8,128)}) %reduce-scatter.2.cloned.1.call-update) | async-done | bytes 262160 | tf_op jit(solution)/shard_map/reduce_scatter | solution.py:40
  167.4 1.7 broadcast_multiply_fusion
  (2 shorter events, 0.0 us)
Async XLA Ops:
  7.2 1.5 copy-start
  7.2 160.2 %reduce-scatter.2.cloned.1.call-start = ((), (), s32[]{:S(2)}) async-start(), calls=%async_computation.1 | async-start | bytes 8650752 | tf_op jit(solution)/shard_map/reduce_scatter | solution.py:40
  14.2 0.9 copy-start.1
  14.2 0.9 copy-start.2
Sparse Core Ops, SparseCore 0:
  14.3 153.0 reduce-scatter.1
where the time goes:
time: 176 us
  waiting for transfers between devices  103 us (59%)
  blocking collectives  44 us (25%)
  between operations  14.1 us (8%)
  matrix products  9.36 us (5%)
  other arithmetic  4.27 us (2%)
    reduce_scatter x1, waiting for transfers between devices, per_device(): lax.psum_scatter(weight_partial, 'dp', scatter_dimension=0, tiled=True)  103 us
    psum x1, blocking collectives, per_device(): gain_grad = lax.psum(gain_local, ('dp', 'tensor')) * factor  44 us
    dot_general x1, matrix products, per_device(): lax.dot_general(normed, grad_kv, (((0,), (0,)), ((), ())), preferred_elem...  5.52 us
    dot_general x1, matrix products, per_device(): lax.dot_general(grad_kv, up_weight, (((1,), (1,)), ((), ())), preferred_e...  3.83 us
  transfers between devices with their start and end apart: 1, of which 1 were waited for; matrix products, arithmetic and copies ran while one was open for 3% of the time, Pallas kernels for 0%

commit v1 on v0

--- a/solution.py
+++ b/solution.py
@@ -1,9 +1,16 @@
+import functools
+
 import jax
 import jax.numpy as jnp
 from jax import lax
+from jax.experimental import pallas as pl
+from jax.experimental.pallas import tpu as pltpu
 from jax.sharding import PartitionSpec as P
 
 epsilon = 1e-06
+MESH = pl.DeviceIdType.MESH
+CHUNKS = 4
+LAG = 1
 
 
 def normalize(latent_raw):
@@ -41,9 +48,291 @@
     return (latent_grad, gain_grad, weight_grad)
 
 
+def kernel(
+    planes, factor, latent_ref, gain_ref, weight_hbm, grad_hbm,
+    latent_out, gain_out, weight_out,
+    own_grad, peer_grad, weight, turned, peer_turned, left,
+    send_one, recv_one, keep_one, send_two, recv_two, keep_two,
+    send_three, recv_three, keep_three, grad_norm, gain_send, gain_recv,
+    load_sem, weight_sem, turned_sem, grad_send_sem, grad_recv_sem,
+    one_send_sem, one_recv_sem, two_send_sem, two_recv_sem,
+    three_send_sem, three_recv_sem, gain_send_sem, gain_recv_sem,
+):
+    units, _, width = own_grad.shape
+    chunks = units // 2
+    rows = weight_out.shape[0]
+    me = lax.axis_index("dp")
+    core, x, y, z = me % 2, (me // 2) % 2, (me // 4) % 2, me // 8
+    partner = me + 1 - 2 * core
+    over_x = me + 2 - 4 * x
+    over_y = me + 4 - 8 * y
+    others = [(z + step) % planes for step in range(1, planes)]
+    peers = [partner, over_x, over_y] + [other * 8 + me % 8 for other in others]
+
+    def columns(unit):
+        return pl.ds(unit * width, width)
+
+    def send(source, target, send_sem, recv_sem, device):
+        return pltpu.make_async_remote_copy(
+            src_ref=source, dst_ref=target, send_sem=send_sem, recv_sem=recv_sem,
+            device_id={"dp": device}, device_id_type=MESH,
+        )
+
+    order = [half * chunks + chunk for chunk in range(chunks) for half in range(2)]
+    loads = {}
+    for unit in order:
+        loads[unit] = pltpu.make_async_copy(
+            grad_hbm.at[:, columns(unit)], own_grad.at[unit], load_sem.at[unit]
+        )
+        loads[unit].start()
+    weight_loads = {}
+    for unit in order:
+        weight_loads[unit] = pltpu.make_async_copy(
+            weight_hbm.at[:, columns(unit)], weight.at[unit], weight_sem.at[unit]
+        )
+        weight_loads[unit].start()
+
+    barrier = pltpu.get_barrier_semaphore()
+    for peer in peers:
+        pl.semaphore_signal(barrier, inc=1, device_id={"dp": peer}, device_id_type=MESH)
+
+    scaled_rows, _ = normalize(latent_ref[...])
+    normed = scaled_rows * gain_ref[...]
+    flipped = normed.T.astype(jnp.bfloat16)
+    flipped = flipped.reshape(planes * 4, 2, rows, flipped.shape[1])
+    turned[0] = flipped[:, 0]
+    turned[1] = flipped[:, 1]
+
+    pl.semaphore_wait(barrier, len(peers))
+
+    grads = {}
+    for position, unit in enumerate(order):
+        loads[unit].wait()
+        grads[unit] = send(
+            own_grad.at[unit], peer_grad.at[unit],
+            grad_send_sem.at[unit], grad_recv_sem.at[unit], partner,
+        )
+        grads[unit].start()
+        if position == 0:
+            turned_copy = send(
+                turned.at[1 - core], peer_turned, turned_sem.at[0], turned_sem.at[1], partner
+            )
+            turned_copy.start()
+
+    def block(plane, away_y, away_x):
+        to_y = (1 - y) if away_y else y
+        to_x = (1 - x) if away_x else x
+        return plane * 4 + to_y * 2 + to_x
+
+    def arrange(side, source):
+        for first in range(2):
+            for second in range(2):
+                for plane in range(planes):
+                    place = (first * 2 + second) * planes + plane
+                    left[0, side, place] = source(block(plane, second == 0, first == 0))
+                    left[1, side, place] = source(block(plane, first == 0, second == 0))
+
+    arrange(0, lambda index: turned[core, index])
+    turned_copy.wait_recv()
+    arrange(1, lambda index: peer_turned[index])
+
+    def left_of(half, side):
+        value = left[half, side]
+        return value.reshape(planes * 4 * rows, value.shape[-1])
+
+    ones, twos, threes = {}, {}, {}
+    half_rows = planes * 2 * rows
+    quarter_rows = planes * rows
+
+    def stage_one(unit):
+        half = unit // chunks
+        grads[unit].wait_recv()
+        partial = jnp.dot(
+            left_of(half, 0), own_grad[unit], preferred_element_type=jnp.float32
+        ) + jnp.dot(left_of(half, 1), peer_grad[unit], preferred_element_type=jnp.float32)
+        send_one[unit] = partial[:half_rows].astype(jnp.bfloat16)
+        keep_one[unit] = partial[half_rows:]
+        ones[unit] = send(
+            send_one.at[unit], recv_one.at[unit],
+            one_send_sem.at[unit], one_recv_sem.at[unit], over_y if half else over_x,
+        )
+        ones[unit].start()
+
+    def stage_two(unit):
+        half = unit // chunks
+        ones[unit].wait_recv()
+        total = keep_one[unit] + recv_one[unit].astype(jnp.float32)
+        send_two[unit] = total[:quarter_rows].astype(jnp.bfloat16)
+        keep_two[unit] = total[quarter_rows:]
+        twos[unit] = send(
+            send_two.at[unit], recv_two.at[unit],
+            two_send_sem.at[unit], two_recv_sem.at[unit], over_x if half else over_y,
+        )
+        twos[unit].start()
+
+    def stage_three(unit):
+        twos[unit].wait_recv()
+        total = keep_two[unit] + recv_two[unit].astype(jnp.float32)
+        total = total.reshape(planes, rows, width)
+        send_three[unit] = total.astype(jnp.bfloat16)
+        keep_three[unit] = total
+        for index, other in enumerate(others):
+            threes[unit, index] = send(
+                send_three.at[unit, other], recv_three.at[unit, z],
+                three_send_sem.at[unit, other], three_recv_sem.at[unit, z], other * 8 + me % 8,
+            )
+            threes[unit, index].start()
+
+    def arrival(unit, other):
+        return send(
+            send_three.at[unit, other], recv_three.at[unit, other],
+            three_send_sem.at[unit, other], three_recv_sem.at[unit, other], other * 8 + me % 8,
+        )
+
+    def finish(unit):
+        total = keep_three[unit, z]
+        for other in others:
+            arrival(unit, other).wait_recv()
+            total = total + recv_three[unit, other].astype(jnp.float32)
+        weight_out[:, columns(unit)] = total * factor
+
+    def norm_part(unit, first):
+        weight_loads[unit].wait()
+        product = lax.dot_general(
+            own_grad[unit], weight[unit], (((1,), (1,)), ((), ())),
+            preferred_element_type=jnp.float32,
+        )
+        grad_norm[...] = product if first else grad_norm[...] + product
+
+    gains = []
+
+    def gain_exchange(stage, value, device):
+        gain_send[stage] = value
+        copy = send(
+            gain_send.at[stage], gain_recv.at[stage],
+            gain_send_sem.at[stage], gain_recv_sem.at[stage], device,
+        )
+        copy.start()
+        gains.append(copy)
+
+    def gain_take(stage):
+        gains[stage].wait_recv()
+        return gain_send[stage] + gain_recv[stage]
+
+    def norm_rest():
+        scaled, inverse = normalize(latent_ref[...])
+        grads_here = grad_norm[...]
+        gain_exchange(0, jnp.sum(grads_here * scaled, axis=0, keepdims=True), partner)
+        latent_out[...] = norm_backward(grads_here, scaled, inverse, gain_ref[...])
+
+    def both(stage, chunk):
+        if 0 <= chunk < chunks:
+            stage(chunk)
+            stage(chunks + chunk)
+
+    for turn in range(chunks + 3 * LAG):
+        both(stage_one, turn)
+        if turn == chunks - 1:
+            for position, unit in enumerate(order):
+                norm_part(unit, position == 0)
+            norm_rest()
+        both(stage_two, turn - LAG)
+        if turn == chunks:
+            gain_exchange(1, gain_take(0), over_x)
+        both(stage_three, turn - 2 * LAG)
+        if turn == chunks + LAG:
+            gain_exchange(2, gain_take(1), over_y)
+        both(finish, turn - 3 * LAG)
+
+    total_gain = gain_take(2)
+    gain_send[3] = total_gain
+    gain_recv[3 + z] = total_gain
+    last = []
+    for index, other in enumerate(others):
+        copy = send(
+            gain_send.at[3], gain_recv.at[3 + z],
+            gain_send_sem.at[3 + index], gain_recv_sem.at[3 + z], other * 8 + me % 8,
+        )
+        copy.start()
+        last.append(copy)
+    for index, other in enumerate(others):
+        send(
+            gain_send.at[3], gain_recv.at[3 + other],
+            gain_send_sem.at[3 + index], gain_recv_sem.at[3 + other], other * 8 + me % 8,
+        ).wait_recv()
+    total_gain = gain_recv[3]
+    for plane in range(1, planes):
+        total_gain = total_gain + gain_recv[3 + plane]
+    gain_out[...] = total_gain * factor
+
+    turned_copy.wait_send()
+    for group in (grads, ones, twos, threes):
+        for copy in group.values():
+            copy.wait_send()
+    for copy in gains + last:
+        copy.wait_send()
+
+
+def fused(latent_raw, norm_gain, up_weight, grad_kv):
+    devices = lax.axis_size("dp")
+    planes = devices // 8
+    tokens, latent_width = latent_raw.shape
+    total_columns = grad_kv.shape[1]
+    units = 2 * CHUNKS
+    width = total_columns // units
+    rows = latent_width // devices
+    factor = float(tokens * devices) ** (-0.5)
+    half_rows, quarter_rows = planes * 2 * rows, planes * rows
+    bf16, f32 = jnp.bfloat16, jnp.float32
+    dma = pltpu.SemaphoreType.DMA
+    vmem = pl.BlockSpec(memory_space=pltpu.VMEM)
+    hbm = pl.BlockSpec(memory_space=pl.ANY)
+    latent_grad, gain_grad, weight_grad = pl.pallas_call(
+        functools.partial(kernel, planes, factor),
+        out_shape=(
+            jax.ShapeDtypeStruct((tokens, latent_width), bf16),
+            jax.ShapeDtypeStruct((1, latent_width), f32),
+            jax.ShapeDtypeStruct((rows, total_columns), f32),
+        ),
+        in_specs=[vmem, vmem, hbm, hbm],
+        out_specs=(vmem, vmem, vmem),
+        scratch_shapes=[
+            pltpu.VMEM((units, tokens, width), bf16),
+            pltpu.VMEM((units, tokens, width), bf16),
+            pltpu.VMEM((units, latent_width, width), bf16),
+            pltpu.VMEM((2, planes * 4, rows, tokens), bf16),
+            pltpu.VMEM((planes * 4, rows, tokens), bf16),
+            pltpu.VMEM((2, 2, planes * 4, rows, tokens), bf16),
+            pltpu.VMEM((units, half_rows, width), bf16),
+            pltpu.VMEM((units, half_rows, width), bf16),
+            pltpu.VMEM((units, half_rows, width), f32),
+            pltpu.VMEM((units, quarter_rows, width), bf16),
+            pltpu.VMEM((units, quarter_rows, width), bf16),
+            pltpu.VMEM((units, quarter_rows, width), f32),
+            pltpu.VMEM((units, planes, rows, width), bf16),
+            pltpu.VMEM((units, planes, rows, width), bf16),
+            pltpu.VMEM((units, planes, rows, width), f32),
+            pltpu.VMEM((tokens, latent_width), f32),
+            pltpu.VMEM((4, 1, latent_width), f32),
+            pltpu.VMEM((3 + planes, 1, latent_width), f32),
+            dma((units,)), dma((units,)), dma((2,)), dma((units,)), dma((units,)),
+            dma((units,)), dma((units,)), dma((units,)), dma((units,)),
+            dma((units, planes)), dma((units, planes)),
+            dma((3 + planes,)), dma((3 + planes,)),
+        ],
+        compiler_params=pltpu.CompilerParams(
+            collective_id=0, has_side_effects=True, vmem_limit_bytes=48 * 1024 * 1024
+        ),
+    )(latent_raw, norm_gain.reshape(1, latent_width), up_weight, grad_kv)
+    return (latent_grad, gain_grad.reshape(latent_width), weight_grad)
+
+
 def solution(mesh):
+    devices = mesh.shape["dp"]
+    covered = mesh.shape["tensor"] == 1 and devices % 8 == 0 and 16 <= devices <= 32
     in_specs = (P("dp", None), P(), P(None, "tensor"), P("dp", "tensor"))
     out_specs = (P("dp", None), P(), P("dp", "tensor"))
     return jax.shard_map(
-        per_device, mesh=mesh, in_specs=in_specs, out_specs=out_specs, check_vma=False
+        fused if covered else per_device,
+        mesh=mesh, in_specs=in_specs, out_specs=out_specs, check_vma=False,
     )

time: 176 us -> 43.4 us (0.25)
  waiting for transfers between devices: 103 us -> 0 us
  blocking collectives: 44 us -> 0 us
  Pallas kernels: 0 us -> 37.6 us
  between operations: 14.1 us -> 0.65 us
  matrix products: 9.36 us -> 0 us
  other arithmetic: 4.27 us -> 0 us
  local copies, waits for them, and re-layouts: 1.19 us -> 4.97 us
    reduce_scatter x1 -> x0, waiting for transfers between devices: 103 us -> none  [per_device(): lax.psum_scatter(weight_partial, 'dp', scatter_dimension=0, tiled=True)]
    psum x1 -> x0, blocking collectives: 44 us -> none  [per_device(): gain_grad = lax.psum(gain_local, ('dp', 'tensor')) * factor]
    pallas_call x0 -> x1, Pallas kernels: none -> 37.6 us  [fused(): pl.pallas_call(functools.partial(kernel, planes, factor), out_shape=(jax....]
    dot_general x2 -> x0, matrix products: 9.36 us -> none  [the longest x1 5.52 us: per_device(): lax.dot_general(normed, grad_kv, (((0,), (0,)), ((), ())), preferred_elem...]
    unnamed x6 -> x9, local copies, waits for them, and re-layouts: 1.19 us -> 4.97 us
    mul x2 -> x0, other arithmetic: 2.25 us -> none  [the longest x1 1.67 us: per_device(): lax.psum_scatter(weight_partial, 'dp', scatter_dimension=0, tiled=True)]
  transfers between devices with their start and end apart: 1 -> 0, of which waited for: 1 -> 0; matrix products, arithmetic and copies ran while one was open for 3% -> 0% of each run, Pallas kernels for 0% -> 0%
where the time goes in v1:
time: 43.4 us; the launch traced here: 43.2 us
  Pallas kernels  37.6 us (87%)
  local copies, waits for them, and re-layouts  4.97 us (11%)
  between operations  0.65 us (1%)
    pallas_call x1, Pallas kernels, fused(): pl.pallas_call(functools.partial(kernel, planes, factor), out_shape=(jax....  37.6 us
    unnamed x9, local copies, waits for them, and re-layouts  4.97 us

profile of v1, /device:TPU:0, one launch (start us, length us, event | category | flops | bytes accessed | tf_op | source)
XLA Modules:
  0.0 43.2 jit_solution(17054732004948847993)
XLA Ops:
  0.6 0.0 copy-start
  0.6 1.4 %copy-done = bf16[192,4096]{1,0:T(8,128)(2,1)S(1)} copy-done((bf16[192,4096]{1,0:T(8,128)(2,1)S(1)}, bf16[192,4096]{1,0:T(8,128)(2,1)}, u32[]{:S(2)}) %copy-start) | copy-done | bytes 1572888
  2.0 0.0 copy-start.1
  2.0 0.9 %copy-done.1 = bf16[192,512]{1,0:T(8,128)(2,1)S(1)} copy-done((bf16[192,512]{1,0:T(8,128)(2,1)S(1)}, bf16[192,512]{1,0:T(8,128)(2,1)}, u32[]{:S(2)}) %copy-start.1) | copy-done | bytes 196632
  3.0 0.0 copy-start.2
  3.0 0.7 %copy-done.2 = f32[512]{0:T(512)S(1)} copy-done((f32[512]{0:T(512)S(1)}, f32[512]{0:T(512)}, u32[]{:S(2)}) %copy-start.2) | copy-done | bytes 2072
  3.6 37.6 %shard_map.67 = (bf16[192,512]{1,0:T(8,128)(2,1)S(1)}, f32[1,512]{1,0:T(1,128)S(1)}, f32[16,4096]{1,0:T(8,128)S(1)}) custom-call(bf16[192,512]{1,0:T(8,128)(2,1)S(1)} %copy-done.1, f32[1,512]{1,0:T(1,128)S(1)} %bitcast.2, bf16[512,4096]{1,0:T(8,128)(2,1)} %weight_hbm.1, bf16[192,4096]{1,0:T(8,128)(2,1)S(1)} %copy-done), custom_call_target="tpu_custom_call" | custom-call | tf_op jit(solution)/shard_map/pallas_call | solution.py:290
  41.2 0.7 %copy.10 = bf16[192,512]{1,0:T(8,128)(2,1)} copy(bf16[192,512]{1,0:T(8,128)(2,1)S(1)} %get-tuple-element.12) | data formatting | bytes 393216
  41.9 0.6 %copy.11 = f32[512]{0:T(512)} copy(f32[512]{0:T(512)S(1)} %bitcast.3) | data formatting | bytes 4096
  42.5 0.7 %copy.12 = f32[16,4096]{1,0:T(8,128)} copy(f32[16,4096]{1,0:T(8,128)S(1)} %get-tuple-element.14) | data formatting | bytes 524288
Async XLA Ops:
  0.6 1.4 %copy-start = (bf16[192,4096]{1,0:T(8,128)(2,1)S(1)}, bf16[192,4096]{1,0:T(8,128)(2,1)}, u32[]{:S(2)}) copy-start(bf16[192,4096]{1,0:T(8,128)(2,1)} %grad_hbm.1) | copy-start | bytes 4718596
  2.0 0.9 %copy-start.1 = (bf16[192,512]{1,0:T(8,128)(2,1)S(1)}, bf16[192,512]{1,0:T(8,128)(2,1)}, u32[]{:S(2)}) copy-start(bf16[192,512]{1,0:T(8,128)(2,1)} %latent_ref.1) | copy-start | bytes 589828
  3.0 0.7 %copy-start.2 = (f32[512]{0:T(512)S(1)}, f32[512]{0:T(512)}, u32[]{:S(2)}) copy-start(f32[512]{0:T(512)} %param.5) | copy-start | bytes 6148

commit v2 on v1

--- a/solution.py
+++ b/solution.py
@@ -11,6 +11,8 @@
 MESH = pl.DeviceIdType.MESH
 CHUNKS = 4
 LAG = 1
+NORM_TURN = 1
+GAIN_STEP = 1
 
 
 def normalize(latent_raw):
@@ -49,12 +51,12 @@
 
 
 def kernel(
-    planes, factor, latent_ref, gain_ref, weight_hbm, grad_hbm,
-    latent_out, gain_out, weight_out,
+    planes, factor, latent_hbm, gain_hbm, weight_hbm, grad_hbm,
+    latent_out, gain_out, weight_out, latent_ref, gain_ref,
     own_grad, peer_grad, weight, turned, peer_turned, left,
     send_one, recv_one, keep_one, send_two, recv_two, keep_two,
     send_three, recv_three, keep_three, grad_norm, gain_send, gain_recv,
-    load_sem, weight_sem, turned_sem, grad_send_sem, grad_recv_sem,
+    small_sem, load_sem, weight_sem, turned_sem, grad_send_sem, grad_recv_sem,
     one_send_sem, one_recv_sem, two_send_sem, two_recv_sem,
     three_send_sem, three_recv_sem, gain_send_sem, gain_recv_sem,
 ):
@@ -78,6 +80,12 @@
             device_id={"dp": device}, device_id_type=MESH,
         )
 
+    small_loads = [
+        pltpu.make_async_copy(latent_hbm, latent_ref, small_sem.at[0]),
+        pltpu.make_async_copy(gain_hbm, gain_ref, small_sem.at[1]),
+    ]
+    for copy in small_loads:
+        copy.start()
     order = [half * chunks + chunk for chunk in range(chunks) for half in range(2)]
     loads = {}
     for unit in order:
@@ -96,6 +104,8 @@
     for peer in peers:
         pl.semaphore_signal(barrier, inc=1, device_id={"dp": peer}, device_id_type=MESH)
 
+    for copy in small_loads:
+        copy.wait()
     scaled_rows, _ = normalize(latent_ref[...])
     normed = scaled_rows * gain_ref[...]
     flipped = normed.T.astype(jnp.bfloat16)
@@ -206,23 +216,60 @@
 
     gains = []
 
-    def gain_exchange(stage, value, device):
-        gain_send[stage] = value
+    def gain_send_to(stage, slot, device, at):
         copy = send(
-            gain_send.at[stage], gain_recv.at[stage],
-            gain_send_sem.at[stage], gain_recv_sem.at[stage], device,
+            gain_send.at[stage], gain_recv.at[slot],
+            gain_send_sem.at[at], gain_recv_sem.at[slot], device,
         )
         copy.start()
         gains.append(copy)
 
+    def gain_pair(stage, device):
+        gain_send_to(stage, stage, device, stage)
+
     def gain_take(stage):
-        gains[stage].wait_recv()
+        gains_of[stage].wait_recv()
         return gain_send[stage] + gain_recv[stage]
+
+    gains_of = {}
+
+    def gain_first(value):
+        gain_send[0] = value
+        gain_pair(0, partner)
+        gains_of[0] = gains[-1]
+
+    def gain_planes():
+        value = gain_take(0)
+        gain_send[3] = value
+        gain_recv[3 + z] = value
+        for index, other in enumerate(others):
+            gain_send_to(3, 3 + z, other * 8 + me % 8, 3 + index)
+
+    def gain_over_x():
+        for index, other in enumerate(others):
+            send(
+                gain_send.at[3], gain_recv.at[3 + other],
+                gain_send_sem.at[3 + index], gain_recv_sem.at[3 + other], other * 8 + me % 8,
+            ).wait_recv()
+        value = gain_recv[3]
+        for plane in range(1, planes):
+            value = value + gain_recv[3 + plane]
+        gain_send[1] = value
+        gain_pair(1, over_x)
+        gains_of[1] = gains[-1]
+
+    def gain_over_y():
+        gain_send[2] = gain_take(1)
+        gain_pair(2, over_y)
+        gains_of[2] = gains[-1]
+
+    def gain_end():
+        gain_out[...] = gain_take(2) * factor
 
     def norm_rest():
         scaled, inverse = normalize(latent_ref[...])
         grads_here = grad_norm[...]
-        gain_exchange(0, jnp.sum(grads_here * scaled, axis=0, keepdims=True), partner)
+        gain_first(jnp.sum(grads_here * scaled, axis=0, keepdims=True))
         latent_out[...] = norm_backward(grads_here, scaled, inverse, gain_ref[...])
 
     def both(stage, chunk):
@@ -232,45 +279,50 @@
 
     for turn in range(chunks + 3 * LAG):
         both(stage_one, turn)
-        if turn == chunks - 1:
+        if turn == NORM_TURN:
             for position, unit in enumerate(order):
                 norm_part(unit, position == 0)
             norm_rest()
         both(stage_two, turn - LAG)
-        if turn == chunks:
-            gain_exchange(1, gain_take(0), over_x)
+        if turn == NORM_TURN:
+            gain_planes()
         both(stage_three, turn - 2 * LAG)
-        if turn == chunks + LAG:
-            gain_exchange(2, gain_take(1), over_y)
+        if turn == NORM_TURN + GAIN_STEP:
+            gain_over_x()
+        if turn == NORM_TURN + 2 * GAIN_STEP:
+            gain_over_y()
+        if turn == NORM_TURN + 3 * GAIN_STEP:
+            gain_end()
         both(finish, turn - 3 * LAG)
-
-    total_gain = gain_take(2)
-    gain_send[3] = total_gain
-    gain_recv[3 + z] = total_gain
-    last = []
-    for index, other in enumerate(others):
-        copy = send(
-            gain_send.at[3], gain_recv.at[3 + z],
-            gain_send_sem.at[3 + index], gain_recv_sem.at[3 + z], other * 8 + me % 8,
-        )
-        copy.start()
-        last.append(copy)
-    for index, other in enumerate(others):
-        send(
-            gain_send.at[3], gain_recv.at[3 + other],
-            gain_send_sem.at[3 + index], gain_recv_sem.at[3 + other], other * 8 + me % 8,
-        ).wait_recv()
-    total_gain = gain_recv[3]
-    for plane in range(1, planes):
-        total_gain = total_gain + gain_recv[3 + plane]
-    gain_out[...] = total_gain * factor
 
     turned_copy.wait_send()
     for group in (grads, ones, twos, threes):
         for copy in group.values():
             copy.wait_send()
-    for copy in gains + last:
+    for copy in gains:
         copy.wait_send()
+
+
+def place_kernel(first_in, second_in, third_in, first_out, second_out, third_out, sem):
+    pairs = ((first_in, first_out), (second_in, second_out), (third_in, third_out))
+    copies = [pltpu.make_async_copy(*pair, sem.at[at]) for at, pair in enumerate(pairs)]
+    for copy in copies:
+        copy.start()
+    for copy in copies:
+        copy.wait()
+
+
+def place(*arrays):
+    hbm = pl.BlockSpec(memory_space=pl.ANY)
+    vmem = pl.BlockSpec(memory_space=pltpu.VMEM)
+    return pl.pallas_call(
+        place_kernel,
+        out_shape=tuple(jax.ShapeDtypeStruct(a.shape, a.dtype) for a in arrays),
+        in_specs=[vmem] * 3,
+        out_specs=(hbm,) * 3,
+        scratch_shapes=[pltpu.SemaphoreType.DMA((3,))],
+        compiler_params=pltpu.CompilerParams(vmem_limit_bytes=8 * 1024 * 1024),
+    )(*arrays)
 
 
 def fused(latent_raw, norm_gain, up_weight, grad_kv):
@@ -290,13 +342,15 @@
     latent_grad, gain_grad, weight_grad = pl.pallas_call(
         functools.partial(kernel, planes, factor),
         out_shape=(
-            jax.ShapeDtypeStruct((tokens, latent_width), bf16),
-            jax.ShapeDtypeStruct((1, latent_width), f32),
-            jax.ShapeDtypeStruct((rows, total_columns), f32),
+            pltpu.VMEM((tokens, latent_width), bf16),
+            pltpu.VMEM((1, latent_width), f32),
+            pltpu.VMEM((rows, total_columns), f32),
         ),
-        in_specs=[vmem, vmem, hbm, hbm],
+        in_specs=[pl.BlockSpec(memory_space=pltpu.HBM)] * 4,
         out_specs=(vmem, vmem, vmem),
         scratch_shapes=[
+            pltpu.VMEM((tokens, latent_width), bf16),
+            pltpu.VMEM((1, latent_width), f32),
             pltpu.VMEM((units, tokens, width), bf16),
             pltpu.VMEM((units, tokens, width), bf16),
             pltpu.VMEM((units, latent_width, width), bf16),
@@ -315,15 +369,16 @@
             pltpu.VMEM((tokens, latent_width), f32),
             pltpu.VMEM((4, 1, latent_width), f32),
             pltpu.VMEM((3 + planes, 1, latent_width), f32),
-            dma((units,)), dma((units,)), dma((2,)), dma((units,)), dma((units,)),
+            dma((2,)), dma((units,)), dma((units,)), dma((2,)), dma((units,)), dma((units,)),
             dma((units,)), dma((units,)), dma((units,)), dma((units,)),
             dma((units, planes)), dma((units, planes)),
             dma((3 + planes,)), dma((3 + planes,)),
         ],
         compiler_params=pltpu.CompilerParams(
-            collective_id=0, has_side_effects=True, vmem_limit_bytes=48 * 1024 * 1024
+            collective_id=0, has_side_effects=True, vmem_limit_bytes=67043328 - 512 * 1024
         ),
     )(latent_raw, norm_gain.reshape(1, latent_width), up_weight, grad_kv)
+    latent_grad, gain_grad, weight_grad = place(latent_grad, gain_grad, weight_grad)
     return (latent_grad, gain_grad.reshape(latent_width), weight_grad)
 
 

time: 43.4 us -> 36 us (0.83)
  local copies, waits for them, and re-layouts: 4.97 us -> 0 us
  Pallas kernels: 37.6 us -> 35.2 us
    unnamed x9 -> x0, local copies, waits for them, and re-layouts: 4.97 us -> none
    pallas_call x1 -> x2, Pallas kernels: 37.6 us -> 35.2 us  [the longest x1 34.4 us: fused(): pl.pallas_call(functools.partial(kernel, planes, factor), out_shape=(pltp...]
where the time goes in v2:
time: 36 us; the launch traced here: 35.9 us
  Pallas kernels  35.2 us (98%)
  between operations  0.64 us (2%)
    pallas_call x1, Pallas kernels, fused(): pl.pallas_call(functools.partial(kernel, planes, factor), out_shape=(pltp...  34.4 us
    pallas_call x1, Pallas kernels, place(): pl.pallas_call(place_kernel, out_shape=tuple((jax.ShapeDtypeStruct(a.shap...  0.8 us

profile of v2, /device:TPU:0, one launch (start us, length us, event | category | flops | bytes accessed | tf_op | source)
XLA Modules:
  0.0 35.9 jit_solution(9630876378333705689)
XLA Ops:
  0.6 34.4 %shard_map.67 = (bf16[192,512]{1,0:T(8,128)(2,1)S(1)}, f32[1,512]{1,0:T(1,128)S(1)}, f32[16,4096]{1,0:T(8,128)S(1)}) custom-call(bf16[192,512]{1,0:T(8,128)(2,1)} %latent_hbm.1, f32[1,512]{1,0:T(1,128)} %bitcast.2, bf16[512,4096]{1,0:T(8,128)(2,1)} %weight_hbm.1, bf16[192,4096]{1,0:T(8,128)(2,1)} %grad_hbm.1), custom_call_target="tpu_custom_call" | custom-call | tf_op jit(solution)/shard_map/pallas_call | solution.py:342
  35.1 0.8 %shard_map.68 = (bf16[192,512]{1,0:T(8,128)(2,1)}, f32[1,512]{1,0:T(1,128)}, f32[16,4096]{1,0:T(8,128)}) custom-call(bf16[192,512]{1,0:T(8,128)(2,1)S(1)} %get-tuple-element.9.first_in, f32[1,512]{1,0:T(1,128)S(1)} %get-tuple-element.10.second_in, f32[16,4096]{1,0:T(8,128)S(1)} %get-tuple-element.11.third_in), custom_call_target="tpu_custom_call" | custom-call | tf_op jit(solution)/shard_map/pallas_call | solution.py:318
